TPU v7x, 128 devices: a whole 4x4x4 slice. The times are simulated.
128 devices in a mesh: rows: 4 (over z_hi, core), cols: 32 (over x, z_lo, y).
Axes of the slice: x: 4, y: 4, z: 4 (z_hi: 2, z_lo: 2; z = z_hi * 2 + z_lo), core: 2. Of those that a mesh axis runs over, the one named last changes fastest.
Arguments:
- tokens: bfloat16 [2048, 6144], P('rows', 'cols'), may hold values from -6 to 6
- cotangent: bfloat16 [2048, 16384], P('rows', 'cols'), may hold values from -0.049804688 to 0.049804688
- weight: bfloat16 [6144, 16384], P(None, 'cols'), may hold values from -6 to 6
- momentum: float32 [128, 768, 1024], P(('rows', 'cols')), may hold values from -40 to 40
Outputs:
- new_weight: bfloat16 [6144, 16384], P(None, 'cols')
- input_grad: bfloat16 [2048, 6144], P('rows', 'cols')
- new_momentum: float32 [128, 768, 1024], P(('rows', 'cols'))
- update: float32 [128, 768, 1024], P(('rows', 'cols'))
All inputs are finite; a program needn't handle non-finite values.
Results may differ from a plain program's by a relative error of at most 0.012.
Values may be sent and summed in bfloat16 or wider, within the bound.
A program may use at most 128 MiB of HBM per device.

v0:
```python
import jax
import jax.numpy as jnp
from jax import lax
from jax.sharding import Mesh
from jax.sharding import PartitionSpec as P

NS_STEPS = 2
COLS = ("cols_0", "cols_1", "cols_2")
ROWS_COLS = ("rows", "cols_0", "cols_1", "cols_2")
coef_a = 3.4445
coef_b = -4.775
coef_c = 2.0315
beta_mom = 0.95
step_rate = 0.25


def reduced_to_own(pieces, axes, sequence):
    inside = pieces.shape[1:]
    pieces = pieces.reshape(*(lax.axis_size(a) for a in axes), *inside)
    pieces = jnp.moveaxis(pieces, sequence, range(len(axes))).reshape(-1, *inside)
    for k in sequence:
        pieces = lax.psum_scatter(pieces, axes[k], scatter_dimension=0, tiled=True)
    return pieces[0]


def cut_along(x, dim, count):
    before, after = (x.shape[:dim], x.shape[dim + 1 :])
    return jnp.moveaxis(x.reshape(*before, count, -1, *after), dim, 0)


def summed_rows(x, axes, sequence, dim):
    count = lax.axis_size(axes)
    return reduced_to_own(cut_along(x, dim, count), axes, sequence)


def partner(x, axis, bit):
    return lax.ppermute(x, axis, [(i, i ^ 1 << bit) for i in range(lax.axis_size(axis))])


def orthogonalize(matrix):
    norm_value = jnp.sqrt(jnp.sum(matrix * matrix))
    current = (matrix / (norm_value + 1e-07)).astype(jnp.bfloat16)
    for index in range(NS_STEPS):
        square = jnp.dot(current, current.T, preferred_element_type=jnp.float32).astype(
            jnp.bfloat16
        )
        poly = (
            coef_b * square.astype(jnp.float32)
            + coef_c * jnp.dot(square, square, preferred_element_type=jnp.float32)
        ).astype(jnp.bfloat16)
        current = (
            coef_a * current.astype(jnp.float32)
            + jnp.dot(poly, current, preferred_element_type=jnp.float32)
        ).astype(jnp.bfloat16)
    return current


def body(tokens, cotangent, weight, momentum):
    half_bit = lax.axis_index(COLS) % 2
    other_bit = 1 - half_bit
    groups = lax.axis_size("rows")
    partial_value = lax.dot_general(
        lax.all_gather(tokens, COLS, axis=1, tiled=True),
        cotangent,
        (((0,), (0,)), ((), ())),
        preferred_element_type=jnp.float32,
    )
    terms = lax.dot_general(
        cotangent, weight, (((1,), (1,)), ((), ())), preferred_element_type=jnp.float32
    )
    input_grad = summed_rows(terms, COLS, (0, 2, 1), 1).astype(jnp.bfloat16)
    d_rows, f_cols = partial_value.shape
    block_rows = d_rows // (2 * groups)
    summed = lax.psum_scatter(partial_value, "rows", scatter_dimension=0, tiled=True)
    split = summed.reshape(2, block_rows, f_cols)
    mine = lax.dynamic_index_in_dim(split, half_bit, 0, keepdims=False)
    theirs = lax.dynamic_index_in_dim(split, other_bit, 0, keepdims=False)
    received = partner(theirs, COLS, 0)
    joined = jnp.where(
        half_bit == 0, jnp.concatenate([mine, received], 1), jnp.concatenate([received, mine], 1)
    )
    grad_block = joined[None]
    new_momentum = beta_mom * momentum + grad_block
    block_cols = new_momentum.shape[2]
    scale_value = float(max(block_rows, block_cols)) ** 0.5
    update = scale_value * orthogonalize(new_momentum[0]).astype(jnp.float32)
    sent = update.astype(jnp.bfloat16)
    col_split = sent.reshape(block_rows, 2, f_cols)
    mine = lax.dynamic_index_in_dim(col_split, half_bit, 1, keepdims=False)
    theirs = lax.dynamic_index_in_dim(col_split, other_bit, 1, keepdims=False)
    received = partner(theirs, COLS, 0)
    stacked = jnp.where(
        half_bit == 0, jnp.concatenate([mine, received], 0), jnp.concatenate([received, mine], 0)
    )
    placed = lax.all_gather(stacked, "rows", axis=0, tiled=True)
    new_weight = (weight.astype(jnp.float32) - step_rate * placed.astype(jnp.float32)).astype(
        jnp.bfloat16
    )
    return (new_weight, input_grad, new_momentum, update[None])


def solution(mesh):
    torus = Mesh(
        mesh.devices.reshape(mesh.shape["rows"], 4, 2, 4), ("rows", "cols_0", "cols_1", "cols_2")
    )
    in_specs = (P("rows", COLS), P("rows", COLS), P(None, COLS), P(ROWS_COLS, None, None))
    out_specs = (P(None, COLS), P("rows", COLS), P(ROWS_COLS, None, None), P(ROWS_COLS, None, None))
    return jax.shard_map(body, mesh=torus, in_specs=in_specs, out_specs=out_specs, check_vma=False)
```

profile of v0, /device:TPU:1, one launch (start us, length us, event | category | flops | bytes accessed | tf_op | source)
XLA Modules:
  0.0 557.8 jit_solution(7268899705757204786)
XLA Ops:
  8.0 0.0 all-gather.3.cloned.1.call-start
  8.1 0.7 all-gather.3.cloned.1.call-update
  8.7 0.0 reduce-scatter.7.cloned.1.call-start
  8.8 0.2 copy-done
  9.0 9.2 %fusion.15 = f32[512,6144]{0,1:T(8,128)} fusion(bf16[512,512]{1,0:T(8,128)(2,1)S(1)} %copy-done, bf16[6144,512]{1,0:T(8,128)(2,1)} %param.6), kind=kOutput, calls=%fused_computation.30 | convolution fusion | flops 3221225472 | bytes 19398656 | tf_op jit(solution)/shard_map/dot_general | solution.py:68
  18.3 11.6 %copy.15 = f32[4,4,2,512,192]{3,4,2,1,0:T(8,128)} copy(f32[4,4,2,512,192]{3,4,1,2,0:T(8,128)} %bitcast.40) | data formatting | bytes 25165824 | tf_op jit(solution)/shard_map/transpose | solution.py:20
  29.9 0.0 reduce-scatter.5.cloned.1.call-start
  29.9 214.0 %all-gather.3.cloned.1.call-done = bf16[512,6144]{0,1:T(8,128)(2,1)} async-done(((bf16[512,192]{0,1:T(8,128)(2,1)}), bf16[512,6144]{0,1:T(8,128)(2,1)}) %all-gather.3.cloned.1.call-update) | async-done | bytes 6291472 | tf_op jit(solution)/shard_map/all_gather | solution.py:63
  244.0 9.2 %fusion.14 = f32[6144,512]{1,0:T(8,128)} fusion(bf16[512,6144]{0,1:T(8,128)(2,1)} %all-gather.3.cloned.1.call-done, bf16[512,512]{1,0:T(8,128)(2,1)S(1)} %copy-done), kind=kOutput, calls=%fused_computation.29 | convolution fusion | flops 3221225472 | bytes 19398656 | tf_op jit(solution)/shard_map/dot_general | solution.py:62
  253.2 0.0 reduce-scatter.9.cloned.1.call-start
  253.3 0.5 reduce-scatter.9.cloned.1.call-update
  253.8 0.0 reduce-scatter.11.cloned.1.call-start
  253.8 121.0 %reduce-scatter.5.cloned.1.call-done = f32[1536,512]{1,0:T(8,128)} async-done(((f32[6144,512]{1,0:T(8,128)}), f32[1536,512]{1,0:T(8,128)}) %reduce-scatter.5.cloned.1.call-update) | async-done | bytes 3145744 | tf_op jit(solution)/shard_map/reduce_scatter | solution.py:74
  374.9 3.3 dynamic-slice_bitcast_fusion
  378.2 1.2 collective-permute-start
  379.4 59.6 %reduce-scatter.9.cloned.1.call-done = f32[2,512,192]{1,2,0:T(8,128)} async-done(((f32[8,512,192]{1,2,0:T(8,128)}), f32[2,512,192]{1,2,0:T(8,128)}) %reduce-scatter.9.cloned.1.call-update) | async-done | bytes 786448 | tf_op jit(solution)/shard_map/reduce_scatter | solution.py:22
  439.1 0.2 all-gather.5.cloned.1.call-start
  439.3 6.2 %multiply_reduce_fusion = (f32[]{:T(128)}, f32[1,768,1024]{2,1,0:T(8,128)}) fusion(f32[1,768,512]{2,1,0:T(8,128)S(1)} %get-tuple-element.7, f32[1,768,512]{2,1,0:T(8,128)} %bitcast.2, pred[]{:T(512)S(6)} %eq.6, f32[1,768,1024]{2,1,0:T(8,128)} %param.7), kind=kLoop, calls=%fused_computation.9 | loop fusion | flops 5505023 | bytes 9437189 | tf_op jit(solution)/shard_map/reduce_sum | solution.py:41
  446.2 4.3 fusion.6
  450.5 5.2 add_convert_fusion.1
  455.7 1.4 convolution_convert_fusion
  457.2 4.6 fusion.1
  461.7 2.9 reshape.82
  464.6 3.2 constant_dynamic-slice_fusion.1
  467.8 0.2 copy.21
  468.1 1.3 collective-permute-start.1
  469.3 0.2 copy.22
  469.5 16.6 %collective-permute-done.1 = bf16[768,512]{1,0:T(8,128)(2,1)S(1)} collective-permute-done((bf16[768,512]{1,0:T(8,128)(2,1)S(1)}, bf16[768,512]{1,0:T(8,128)(2,1)S(1)}, u32[]{:S(2)}, u32[]{:S(2)}) %collective-permute-start.1) | collective-permute-done | bytes 786464 | tf_op jit(solution)/shard_map/ppermute | solution.py:37
  486.1 1.8 maximum_select_fusion.1
  488.0 1.7 convert_bitcast_fusion
  489.7 51.3 %all-gather.5.cloned.1.call-done = bf16[6144,512]{1,0:T(8,128)(2,1)} async-done(((bf16[1536,512]{1,0:T(8,128)(2,1)}), bf16[6144,512]{1,0:T(8,128)(2,1)}) %all-gather.5.cloned.1.call-update) | async-done | bytes 6291472 | tf_op jit(solution)/shard_map/all_gather | solution.py:95
  541.0 9.2 %subtract_convert_fusion = bf16[6144,512]{1,0:T(8,128)(2,1)} fusion(bf16[6144,512]{1,0:T(8,128)(2,1)} %all-gather.5.cloned.1.call-done, bf16[6144,512]{1,0:T(8,128)(2,1)} %param.6), kind=kLoop, calls=%fused_computation | loop fusion | flops 15728640 | bytes 18874368 | tf_op jit(solution)/shard_map/convert_element_type | solution.py:96
  (10 shorter events, 0.1 us)
Async XLA Ops:
  8.0 1.1 copy-start
  8.0 236.0 %all-gather.3.cloned.1.call-start = ((), (), s32[]{:S(2)}) async-start(), calls=%async_computation.4 | async-start | bytes 6488064 | tf_op jit(solution)/shard_map/all_gather | solution.py:63
  8.7 244.5 %reduce-scatter.7.cloned.1.call-start = ((), (), s32[]{:S(2)}) async-start(), calls=%async_computation.7 | async-start | bytes 15728640 | tf_op jit(solution)/shard_map/reduce_scatter | solution.py:22
  29.9 345.0 %reduce-scatter.5.cloned.1.call-start = ((), (), s32[]{:S(2)}) async-start(), calls=%async_computation.5 | async-start | bytes 15728640 | tf_op jit(solution)/shard_map/reduce_scatter | solution.py:74
  253.2 185.8 %reduce-scatter.9.cloned.1.call-start = ((), (), s32[]{:S(2)}) async-start(), calls=%async_computation.8 | async-start | bytes 3932160 | tf_op jit(solution)/shard_map/reduce_scatter | solution.py:22
  253.8 234.2 %reduce-scatter.11.cloned.1.call-start = ((), (), s32[]{:S(2)}) async-start(), calls=%async_computation.9 | async-start | bytes 1179648 | tf_op jit(solution)/shard_map/reduce_scatter | solution.py:22
  378.2 61.1 %collective-permute-start = (f32[768,512]{1,0:T(8,128)}, f32[768,512]{1,0:T(8,128)}, u32[]{:S(2)}, u32[]{:S(2)}) collective-permute-start(f32[768,512]{1,0:T(8,128)} %get-tuple-element.6), channel_id=1, source_target_pairs={{0,1},{1,0},{2,3},{3,2},{4,5},{5,4},{6,7},{7,6},{8,9},{9,8},{10,11... | collective-permute-start | bytes 4718600 | tf_op jit(solution)/shard_map/ppermute | solution.py:37
  439.1 102.0 %all-gather.5.cloned.1.call-start = ((), (), s32[]{:S(2)}) async-start(), calls=%async_computation.6 | async-start | bytes 7864320 | tf_op jit(solution)/shard_map/all_gather | solution.py:95
  468.1 18.1 %collective-permute-start.1 = (bf16[768,512]{1,0:T(8,128)(2,1)S(1)}, bf16[768,512]{1,0:T(8,128)(2,1)S(1)}, u32[]{:S(2)}, u32[]{:S(2)}) collective-permute-start(bf16[768,512]{1,0:T(8,128)(2,1)S(1)} %bitcast.44), channel_id=1, source_target_pairs={{0,1},{1,0},{2,3},{3,2},{4,5},{5,4},{6,7},{7,6},{8,9},{9,8},{10,11... | collective-permute-start | bytes 2359304 | tf_op jit(solution)/shard_map/ppermute | solution.py:37
  541.0 9.2 %copy-start.1 = (bf16[512,512]{1,0:T(8,128)(2,1)S(1)}, bf16[512,512]{1,0:T(8,128)(2,1)}, u32[]{:S(2)}) copy-start(bf16[512,512]{1,0:T(8,128)(2,1)} %param.5) | copy-start | bytes 1572868
Sparse Core Ops, SparseCore 0:
  10.5 233.4 all-gather.2
Sparse Core Ops, SparseCore 1:
  30.0 128.8 reduce-scatter.6
  253.3 121.6 reduce-scatter.4
  377.2 61.8 reduce-scatter.8
  441.4 20.1 reduce-scatter.10
  488.1 52.9 all-gather.4
where the time goes:
time: 558 us
  waiting for transfers between devices  464 us (83%)
  matrix products  33.9 us (6%)
  local copies, waits for them, and re-layouts  21.7 us (4%)
  other arithmetic  18.9 us (3%)
  between operations  16.5 us (3%)
    all_gather x1, waiting for transfers between devices, body(): lax.all_gather(tokens, COLS, axis=1, tiled=True)  214 us
    reduce_scatter x1, waiting for transfers between devices, body(): lax.psum_scatter(partial_value, 'rows', scatter_dimension=0, tiled=True)  121 us
    reduce_scatter x3, waiting for transfers between devices, reduced_to_own(): pieces = lax.psum_scatter(pieces, axes[k], scatter_dimension=0, tiled=True)  59.7 us
    all_gather x1, waiting for transfers between devices, body(): placed = lax.all_gather(stacked, 'rows', axis=0, tiled=True)  51.3 us
    ppermute x2, waiting for transfers between devices, partner(): lax.ppermute(x, axis, [(i, i ^ 1 << bit) for i in range(lax.axis_size(axi...  16.6 us
    transpose x1, local copies, waits for them, and re-layouts, reduced_to_own(): jnp.moveaxis(pieces, sequence, range(len(axes))).reshape(-1, *inside)  11.6 us
  transfers between devices with their start and end apart: 8, of which 5 were waited for; matrix products, arithmetic and copies ran while one was open for 12% of the time, Pallas kernels for 0%

commit v1 on v0

--- a/solution.py
+++ b/solution.py
@@ -12,6 +12,15 @@
 coef_c = 2.0315
 beta_mom = 0.95
 step_rate = 0.25
+
+
+def render_edge(xx):
+    return jnp.concatenate(
+        lax.all_to_all(
+            jnp.stack([xx] * lax.axis_size("rows")), axis_name="rows", split_axis=0, concat_axis=0
+        ),
+        0,
+    )
 
 
 def reduced_to_own(pieces, axes, sequence):
@@ -92,7 +101,7 @@
     stacked = jnp.where(
         half_bit == 0, jnp.concatenate([mine, received], 0), jnp.concatenate([received, mine], 0)
     )
-    placed = lax.all_gather(stacked, "rows", axis=0, tiled=True)
+    placed = render_edge(stacked)
     new_weight = (weight.astype(jnp.float32) - step_rate * placed.astype(jnp.float32)).astype(
         jnp.bfloat16
     )

time: 558 us -> 579 us (1.038)
  other arithmetic: 18.9 us -> 29 us
  starting transfers between devices: 2.9 us -> 8.89 us
    reduce_scatter x3, waiting for transfers between devices: 59.7 us -> 144 us  [reduced_to_own(): pieces = lax.psum_scatter(pieces, axes[k], scatter_dimension=0, tiled=True)]
    all_gather x1, waiting for transfers between devices: 214 us -> 146 us  [body(): lax.all_gather(tokens, COLS, axis=1, tiled=True)]
    all_gather x1 -> x0, waiting for transfers between devices: 51.3 us -> none  [body(): placed = lax.all_gather(stacked, 'rows', axis=0, tiled=True)]
    all_to_all x0 -> x1, waiting for transfers between devices: none -> 45.1 us  [render_edge(): lax.all_to_all(jnp.stack([xx] * lax.axis_size('rows')), axis_name='rows',...]
    reduce_scatter x1, waiting for transfers between devices: 121 us -> 106 us  [body(): lax.psum_scatter(partial_value, 'rows', scatter_dimension=0, tiled=True)]
    mul x0 -> x1, other arithmetic: none -> 9.1 us  [body(): step_rate * placed.astype(jnp.float32)]
    ppermute x2, waiting for transfers between devices: 16.6 us -> 24 us  [partner(): lax.ppermute(x, axis, [(i, i ^ 1 << bit) for i in range(lax.axis_size(axi...]
    all_to_all x0 -> x1, starting transfers between devices: none -> 5.94 us  [render_edge(): lax.all_to_all(jnp.stack([xx] * lax.axis_size('rows')), axis_name='rows',...]
  transfers between devices with their start and end apart: 8 -> 8, of which waited for: 5 -> 6; matrix products, arithmetic and copies ran while one was open for 12% -> 10% of each run, Pallas kernels for 0% -> 0%
where the time goes in v1:
time: 579 us; the launch traced here: 578 us
  waiting for transfers between devices  467 us (81%)
  matrix products  34.2 us (6%)
  other arithmetic  29 us (5%)
  local copies, waits for them, and re-layouts  24.6 us (4%)
  between operations  14.6 us (3%)
  starting transfers between devices  8.89 us (2%)
    all_gather x1, waiting for transfers between devices, body(): lax.all_gather(tokens, COLS, axis=1, tiled=True)  146 us
    reduce_scatter x3, waiting for transfers between devices, reduced_to_own(): pieces = lax.psum_scatter(pieces, axes[k], scatter_dimension=0, tiled=True)  144 us
    reduce_scatter x1, waiting for transfers between devices, body(): lax.psum_scatter(partial_value, 'rows', scatter_dimension=0, tiled=True)  106 us
    all_to_all x1, waiting for transfers between devices, render_edge(): lax.all_to_all(jnp.stack([xx] * lax.axis_size('rows')), axis_name='rows',...  45.1 us
    ppermute x2, waiting for transfers between devices, partner(): lax.ppermute(x, axis, [(i, i ^ 1 << bit) for i in range(lax.axis_size(axi...  24 us
  transfers between devices with their start and end apart: 8, of which 6 were waited for; matrix products, arithmetic and copies ran while one was open for 10% of the time, Pallas kernels for 0%

profile of v1, /device:TPU:1, one launch (start us, length us, event | category | flops | bytes accessed | tf_op | source)
XLA Modules:
  0.0 578.2 jit_solution(624135430914134308)
XLA Ops:
  7.2 0.7 all-gather.2.cloned.1.call-update
  7.9 0.0 reduce-scatter.5.cloned.1.call-start
  8.0 146.2 %all-gather.2.cloned.1.call-done = bf16[512,6144]{0,1:T(8,128)(2,1)} async-done(((bf16[512,192]{0,1:T(8,128)(2,1)}), bf16[512,6144]{0,1:T(8,128)(2,1)}) %all-gather.2.cloned.1.call-update) | async-done | bytes 6291472 | tf_op jit(solution)/shard_map/all_gather | solution.py:72
  154.1 9.3 %fusion.15 = f32[6144,512]{1,0:T(8,128)} fusion(bf16[512,6144]{0,1:T(8,128)(2,1)} %all-gather.2.cloned.1.call-done, bf16[512,512]{1,0:T(8,128)(2,1)S(1)} %copy-done), kind=kOutput, calls=%fused_computation.31 | convolution fusion | flops 3221225472 | bytes 19398656 | tf_op jit(solution)/shard_map/dot_general | solution.py:71
  163.5 0.0 reduce-scatter.7.cloned.1.call-start
  163.5 9.4 %fusion.16 = f32[512,6144]{0,1:T(8,128)} fusion(bf16[512,512]{1,0:T(8,128)(2,1)S(1)} %copy-done, bf16[6144,512]{1,0:T(8,128)(2,1)} %param.6), kind=kOutput, calls=%fused_computation.32 | convolution fusion | flops 3221225472 | bytes 19398656 | tf_op jit(solution)/shard_map/dot_general | solution.py:77
  172.9 11.5 %copy.15 = f32[4,4,2,512,192]{3,4,2,1,0:T(8,128)} copy(f32[4,4,2,512,192]{3,4,1,2,0:T(8,128)} %bitcast.44) | data formatting | bytes 25165824 | tf_op jit(solution)/shard_map/transpose | solution.py:29
  184.4 0.0 reduce-scatter.9.cloned.1.call-start
  184.5 106.4 %reduce-scatter.5.cloned.1.call-done = f32[1536,512]{1,0:T(8,128)} async-done(((f32[6144,512]{1,0:T(8,128)}), f32[1536,512]{1,0:T(8,128)}) %reduce-scatter.5.cloned.1.call-update) | async-done | bytes 3145744 | tf_op jit(solution)/shard_map/reduce_scatter | solution.py:83
  290.8 3.3 dynamic-slice_bitcast_fusion
  294.2 1.2 collective-permute-start
  295.4 111.8 %reduce-scatter.7.cloned.1.call-done = f32[8,512,192]{1,2,0:T(8,128)} async-done(((f32[32,512,192]{1,2,0:T(8,128)}), f32[8,512,192]{1,2,0:T(8,128)}) %reduce-scatter.7.cloned.1.call-update) | async-done | bytes 3145744 | tf_op jit(solution)/shard_map/reduce_scatter | solution.py:31
  407.2 6.3 %multiply_reduce_fusion = (f32[]{:T(128)}, f32[1,768,1024]{2,1,0:T(8,128)}) fusion(f32[1,768,512]{2,1,0:T(8,128)S(1)} %get-tuple-element.7, f32[1,768,512]{2,1,0:T(8,128)} %bitcast.2, pred[]{:T(512)S(6)} %eq.6, f32[1,768,1024]{2,1,0:T(8,128)} %param.7), kind=kLoop, calls=%fused_computation.11 | loop fusion | flops 5505023 | bytes 9437189 | tf_op jit(solution)/shard_map/reduce_sum | solution.py:50
  414.1 4.3 fusion.7
  418.4 5.2 add_convert_fusion.1
  423.7 1.4 convolution_convert_fusion
  425.1 4.6 fusion.2
  429.6 2.9 reshape.101
  432.5 3.2 constant_dynamic-slice_fusion.1
  435.8 0.2 copy.21
  436.0 1.6 collective-permute-start.1
  437.6 0.2 copy.22
  437.8 24.0 %collective-permute-done.1 = bf16[768,512]{1,0:T(8,128)(2,1)S(1)} collective-permute-done((bf16[768,512]{1,0:T(8,128)(2,1)S(1)}, bf16[768,512]{1,0:T(8,128)(2,1)S(1)}, u32[]{:S(2)}, u32[]{:S(2)}) %collective-permute-start.1) | collective-permute-done | bytes 786464 | tf_op jit(solution)/shard_map/ppermute | solution.py:46
  461.8 0.6 maximum_select_fusion.1
  462.4 3.2 stack.2
  465.6 5.9 %all-to-all-start = ((bf16[4,1536,512]{2,1,0:T(8,128)(2,1)}), bf16[4,1536,512]{2,1,0:T(8,128)(2,1)}, u32[]{:S(2)}, u32[]{:S(2)}) async-start(bf16[4,1536,512]{2,1,0:T(8,128)(2,1)} %stack.2), calls=%async_computation.1 | async-start | bytes 12582912 | tf_op jit(solution)/shard_map/all_to_all | solution.py:19
  471.5 0.6 reduce-scatter.11.cloned.1.call-update
  472.1 32.3 %reduce-scatter.11.cloned.1.call-done = f32[1,512,192]{1,2,0:T(8,128)} async-done(((f32[2,512,192]{1,2,0:T(8,128)}), f32[1,512,192]{1,2,0:T(8,128)}) %reduce-scatter.11.cloned.1.call-update) | async-done | bytes 393232 | tf_op jit(solution)/shard_map/reduce_scatter | solution.py:31
  504.4 1.7 convert_bitcast_fusion
  506.1 45.1 %all-to-all-done = bf16[4,1536,512]{2,1,0:T(8,128)(2,1)} async-done(((bf16[4,1536,512]{2,1,0:T(8,128)(2,1)}), bf16[4,1536,512]{2,1,0:T(8,128)(2,1)}, u32[]{:S(2)}, u32[]{:S(2)}) %all-to-all-start) | async-done | bytes 6291488 | tf_op jit(solution)/shard_map/all_to_all | solution.py:19
  551.2 9.1 %convert_multiply_fusion = f32[4,1536,512]{2,1,0:T(8,128)} fusion(bf16[4,1536,512]{2,1,0:T(8,128)(2,1)} %all-to-all-done), kind=kLoop, calls=%fused_computation.2 | loop fusion | flops 6291456 | bytes 18874368 | tf_op jit(solution)/shard_map/mul | solution.py:105
  560.3 11.3 %fusion = bf16[6144,512]{1,0:T(8,128)(2,1)} fusion(f32[4,1536,512]{2,1,0:T(8,128)} %convert_multiply_fusion, bf16[6144,512]{1,0:T(8,128)(2,1)} %param.6), kind=kLoop, calls=%fused_computation.1 | loop fusion | flops 9437184 | bytes 25165824 | tf_op jit(solution)/shard_map/convert_element_type | solution.py:105
  (11 shorter events, 0.1 us)
Async XLA Ops:
  7.2 147.0 %copy-start = (bf16[512,512]{1,0:T(8,128)(2,1)S(1)}, bf16[512,512]{1,0:T(8,128)(2,1)}, u32[]{:S(2)}) copy-start(bf16[512,512]{1,0:T(8,128)(2,1)} %param.5) | copy-start | bytes 1572868
  7.2 146.9 %all-gather.2.cloned.1.call-start = ((), (), s32[]{:S(2)}) async-start(), calls=%async_computation.5 | async-start | bytes 6488064 | tf_op jit(solution)/shard_map/all_gather | solution.py:72
  7.9 282.9 %reduce-scatter.5.cloned.1.call-start = ((), (), s32[]{:S(2)}) async-start(), calls=%async_computation.6 | async-start | bytes 15728640 | tf_op jit(solution)/shard_map/reduce_scatter | solution.py:83
  163.5 243.7 %reduce-scatter.7.cloned.1.call-start = ((), (), s32[]{:S(2)}) async-start(), calls=%async_computation.7 | async-start | bytes 15728640 | tf_op jit(solution)/shard_map/reduce_scatter | solution.py:31
  184.4 287.1 %reduce-scatter.9.cloned.1.call-start = ((), (), s32[]{:S(2)}) async-start(), calls=%async_computation.8 | async-start | bytes 3932160 | tf_op jit(solution)/shard_map/reduce_scatter | solution.py:31
  294.2 113.0 %collective-permute-start = (f32[768,512]{1,0:T(8,128)}, f32[768,512]{1,0:T(8,128)}, u32[]{:S(2)}, u32[]{:S(2)}) collective-permute-start(f32[768,512]{1,0:T(8,128)} %get-tuple-element.6), channel_id=1, source_target_pairs={{0,1},{1,0},{2,3},{3,2},{4,5},{5,4},{6,7},{7,6},{8,9},{9,8},{10,11... | collective-permute-start | bytes 4718600 | tf_op jit(solution)/shard_map/ppermute | solution.py:46
  436.0 25.8 %collective-permute-start.1 = (bf16[768,512]{1,0:T(8,128)(2,1)S(1)}, bf16[768,512]{1,0:T(8,128)(2,1)S(1)}, u32[]{:S(2)}, u32[]{:S(2)}) collective-permute-start(bf16[768,512]{1,0:T(8,128)(2,1)S(1)} %bitcast.48), channel_id=1, source_target_pairs={{0,1},{1,0},{2,3},{3,2},{4,5},{5,4},{6,7},{7,6},{8,9},{9,8},{10,11... | collective-permute-start | bytes 2359304 | tf_op jit(solution)/shard_map/ppermute | solution.py:46
  465.6 85.6 %all-to-all-start = ((bf16[4,1536,512]{2,1,0:T(8,128)(2,1)}), bf16[4,1536,512]{2,1,0:T(8,128)(2,1)}, u32[]{:S(2)}, u32[]{:S(2)}) async-start(bf16[4,1536,512]{2,1,0:T(8,128)(2,1)} %stack.2), calls=%async_computation.1 | async-start | bytes 12582912 | tf_op jit(solution)/shard_map/all_to_all | solution.py:19
  471.5 32.9 %reduce-scatter.11.cloned.1.call-start = ((), (), s32[]{:S(2)}) async-start(), calls=%async_computation.9 | async-start | bytes 1179648 | tf_op jit(solution)/shard_map/reduce_scatter | solution.py:31
  560.3 11.3 %copy-start.1 = (bf16[512,512]{1,0:T(8,128)(2,1)S(1)}, bf16[512,512]{1,0:T(8,128)(2,1)}, u32[]{:S(2)}) copy-start(bf16[512,512]{1,0:T(8,128)(2,1)} %param.5) | copy-start | bytes 1572868
Sparse Core Ops, SparseCore 0:
  9.6 144.4 all-gather.1
  163.6 127.2 reduce-scatter.4
  293.3 113.7 reduce-scatter.6
  409.4 42.2 reduce-scatter.8
  474.4 30.0 reduce-scatter.10
